TPU v7x, 256 devices: a whole 4x4x8 slice. The times are simulated.
256 devices in a mesh: gx: 16 (over z, x_lo), gy: 16 (over y, x_hi, core).
Axes of the slice: x: 4 (x_hi: 2, x_lo: 2; x = x_hi * 2 + x_lo), y: 4, z: 8, core: 2. Of those that a mesh axis runs over, the one named last changes fastest.
Arguments:
- gradient: float32 [2048, 512], P('gx', 'gy'), may hold values from -6 to 6
- stat_old: float32 [2048, 2048], P('gx', 'gy'), may hold values from -1.001 to 1.001, as said below
Outputs:
- statistic: float32 [2048, 2048], P('gx', 'gy')
- inverse_root: float32 [2048, 2048], P('gx', 'gy')
Inputs may be any that keep to these rules, and one draw needn't show every extreme that they name: stat_old is symmetric positive semidefinite with unit diagonal, the Gram matrix of 2048 unit-length rows of 512 entries.
All inputs are finite; a program needn't handle non-finite values.
Results may differ from a plain program's by a relative error of at most 0.0003.
Values sent between devices are 32-bit elements.
A program may use at most 64 MiB of HBM per device.

v0:
```python
import jax
import jax.numpy as jnp
from jax import lax
from jax.sharding import Mesh
from jax.sharding import PartitionSpec as P

GY = ("gy_0", "gy_1", "gy_2")
GX = ("gx_0", "gx_1")
GX_GY = ("gx_0", "gx_1", "gy_0", "gy_1", "gy_2")


def gather_axes(array, axes, dim):
    filled = array
    for number in range(len(axes) - 1, -1, -1):
        filled = lax.all_gather(filled, axes[number], axis=dim, tiled=True)
    return filled


def folded(array, axes, dim, take_in, carry):
    everything = jax.tree.map(lambda part: gather_axes(part, axes, dim), array)
    return take_in(carry, everything, jnp.int32(0))


def spread(array, axes, root):
    array = jnp.where(lax.axis_index(axes) == root, array, jnp.zeros_like(array))
    for axis in axes:
        array = lax.psum(array, axis)
    return array


def over_axes(array, axes):
    for axis in axes:
        array = lax.psum(array, axis)
    return array


def matmul(leading, trailing):
    return jnp.dot(
        leading, trailing, preferred_element_type=jnp.float32, precision=lax.Precision.HIGHEST
    )


def panels(factor_one, factor_two):
    whole_row = lax.all_gather(factor_one, GY, axis=1, tiled=True)

    def accumulate(running, shard_rows, first_row):
        matching = lax.dynamic_slice_in_dim(whole_row, first_row, shard_rows.shape[0], 1)
        return running + matmul(matching, shard_rows)

    empty = jnp.zeros((factor_one.shape[0], factor_two.shape[1]), jnp.float32)
    return folded(factor_two, GX, 0, accumulate, empty)


def product(factor_one, factor_two):
    return panels(factor_one, factor_two)


def local(gradient, stat_old):
    count_rows = lax.axis_size(GX)
    count_cols = lax.axis_size(GY)
    factor = count_rows // count_cols
    piece_width = stat_old.shape[0]
    row_index = lax.axis_index(GX)
    col_index = lax.axis_index(GY)
    panel_rows = lax.all_gather(gradient, GY, axis=1, tiled=True)
    outer_parts = []
    for member in range(factor):
        column_rows = spread(panel_rows, GX, col_index * factor + member)
        outer_parts.append(matmul(panel_rows, column_rows.T))
    outer = jnp.concatenate(outer_parts, axis=1) / panel_rows.shape[1]
    statistic = 0.9 * stat_old + outer
    squares = over_axes(jnp.sum(statistic * statistic), GX_GY)
    divisor = 2.0 * jnp.sqrt(squares / (piece_width * count_rows))
    global_rows = row_index * piece_width + lax.broadcasted_iota(jnp.int32, stat_old.shape, 0)
    global_cols = col_index * (factor * piece_width) + lax.broadcasted_iota(
        jnp.int32, stat_old.shape, 1
    )
    identity = (global_rows == global_cols).astype(jnp.float32)
    normed = statistic / divisor
    first_step = 1.5 * identity - 0.5 * normed
    root_half = product(normed, first_step)
    product_mid = product(first_step, root_half)
    second_step = 1.5 * identity - 0.5 * product_mid
    inverse_root = product(second_step, first_step)
    return (statistic, inverse_root)


def solution(mesh):
    torus = Mesh(mesh.devices.reshape(8, 2, 4, 2, 2), ("gx_0", "gx_1", "gy_0", "gy_1", "gy_2"))
    placed = (P(GX, GY), P(GX, GY))
    return jax.shard_map(
        local, mesh=torus, in_specs=placed, out_specs=(P(GX, GY), P(GX, GY)), check_vma=False
    )
```

profile of v0, /device:TPU:1, one launch (start us, length us, event | category | flops | bytes accessed | tf_op | source)
XLA Modules:
  0.0 435.5 jit_solution(8363940582427046131)
XLA Ops:
  7.2 0.0 copy-start.3
  7.2 0.0 all-reduce.3.cloned.1.call-start
  7.2 0.7 copy-done.3
  7.9 26.8 %all_gather.26 = f32[128,512]{0,1:T(8,128)S(1)} all-gather(f32[128,32]{0,1:T(8,128)S(1)} %copy-done.3), channel_id=1, replica_groups=mesh['gx_0'=8,'gx_1'=2,'gy_0'=4,'gy_1'=2,'gy_2'=2] {'gy_0','gy_1','gy_2'}, dimensions={1}, use_global_device_ids=true | all-gather | bytes 278528 | tf_op jit(solution)/shard_map/all_gather | solution.py:65
  34.6 0.7 broadcast_select_fusion
  35.4 0.0 all-reduce.3.cloned.1.call-update
  35.4 0.0 all-reduce.5.cloned.1.call-start
  35.4 65.4 %all-reduce.3.cloned.1.call-done = f32[128,512]{0,1:T(8,128)} async-done(((f32[128,512]{0,1:T(8,128)}), f32[128,512]{0,1:T(8,128)}) %all-reduce.3.cloned.1.call-update) | async-done | bytes 262160 | tf_op jit(solution)/shard_map/psum | solution.py:27
  100.8 0.0 copy-start.2
  100.8 0.0 all-reduce.5.cloned.1.call-update
  100.8 0.0 all-gather.10.cloned.1.call-start
  100.9 0.8 copy-done.2
  101.6 0.1 copy.4
  101.7 39.7 %all-reduce.5.cloned.1.call-done = f32[128,512]{0,1:T(8,128)} async-done(((f32[128,512]{0,1:T(8,128)}), f32[128,512]{0,1:T(8,128)}) %all-reduce.5.cloned.1.call-update) | async-done | bytes 262160 | tf_op jit(solution)/shard_map/psum | solution.py:27
  141.4 2.1 multiply_reduce_fusion
  143.6 14.6 %psum.51 = f32[]{:T(128)} all-reduce(f32[]{:T(128)} %get-tuple-element.6), channel_id=1, replica_groups=mesh['gx_0'=8,'gx_1'=2,'gy_0'=4,'gy_1'=2,'gy_2'=2] {'gx_0'}, use_global_device_ids=true, to_apply=%region_3.4 | all-reduce | flops 1 | bytes 8 | tf_op jit(solution)/shard_map/psum | solution.py:33
  158.1 4.4 %psum.52 = f32[]{:T(128)} all-reduce(f32[]{:T(128)} %psum.51), channel_id=1, replica_groups=mesh['gx_0'=8,'gx_1'=2,'gy_0'=4,'gy_1'=2,'gy_2'=2] {'gx_1'}, use_global_device_ids=true, to_apply=%region_4.5 | all-reduce | flops 1 | bytes 8 | tf_op jit(solution)/shard_map/psum | solution.py:33
  162.5 9.1 %psum.53 = f32[]{:T(128)} all-reduce(f32[]{:T(128)} %psum.52), channel_id=1, replica_groups=mesh['gx_0'=8,'gx_1'=2,'gy_0'=4,'gy_1'=2,'gy_2'=2] {'gy_0'}, use_global_device_ids=true, to_apply=%region_5.6 | all-reduce | flops 1 | bytes 8 | tf_op jit(solution)/shard_map/psum | solution.py:33
  171.6 5.9 %psum.54 = f32[]{:T(128)} all-reduce(f32[]{:T(128)} %psum.53), channel_id=1, replica_groups=mesh['gx_0'=8,'gx_1'=2,'gy_0'=4,'gy_1'=2,'gy_2'=2] {'gy_1'}, use_global_device_ids=true, to_apply=%region_6.7 | all-reduce | flops 1 | bytes 8 | tf_op jit(solution)/shard_map/psum | solution.py:33
  177.5 11.8 %psum.55 = f32[]{:T(128)} all-reduce(f32[]{:T(128)} %psum.54), channel_id=1, replica_groups=mesh['gx_0'=8,'gx_1'=2,'gy_0'=4,'gy_1'=2,'gy_2'=2] {'gy_2'}, use_global_device_ids=true, to_apply=%region_7.8 | all-reduce | flops 1 | bytes 8 | tf_op jit(solution)/shard_map/psum | solution.py:33
  190.0 0.6 select_subtract_fusion
  190.6 0.0 copy-start.1
  190.6 3.9 all_gather.29
  194.5 0.0 copy-done.1
  194.5 0.0 all-gather.10.cloned.1.call-update
  194.5 0.0 all-gather.8.cloned.1.call-start
  194.6 0.5 all-gather.8.cloned.1.call-update
  195.1 0.0 all-gather.6.cloned.1.call-start
  195.1 0.5 all-gather.6.cloned.1.call-update
  195.7 0.0 all-gather.12.cloned.1.call-start
  195.7 29.4 %all-gather.10.cloned.1.call-done = f32[2048,128]{0,1:T(8,128)} async-done(((f32[256,128]{0,1:T(8,128)}), f32[2048,128]{0,1:T(8,128)}) %all-gather.10.cloned.1.call-update) | async-done | bytes 1048592 | tf_op jit(solution)/shard_map/all_gather | solution.py:15
  225.1 56.8 %all-gather.8.cloned.1.call-done = f32[128,2048]{0,1:T(8,128)} async-done(((f32[128,128]{0,1:T(8,128)}), f32[128,2048]{0,1:T(8,128)}) %all-gather.8.cloned.1.call-update) | async-done | bytes 1048592 | tf_op jit(solution)/shard_map/all_gather | solution.py:44
  281.9 3.4 fusion.3
  285.2 3.9 all_gather.31
  289.1 0.0 all-gather.12.cloned.1.call-update
  289.1 0.0 copy-start
  289.1 0.0 all-gather.14.cloned.1.call-start
  289.2 44.5 %all-gather.6.cloned.1.call-done = f32[128,2048]{0,1:T(8,128)} async-done(((f32[128,128]{0,1:T(8,128)}), f32[128,2048]{0,1:T(8,128)}) %all-gather.6.cloned.1.call-update) | async-done | bytes 1048592 | tf_op jit(solution)/shard_map/all_gather | solution.py:44
  333.7 33.6 %all-gather.12.cloned.1.call-done = f32[2048,128]{1,0:T(8,128)} async-done(((f32[256,128]{1,0:T(8,128)}), f32[2048,128]{1,0:T(8,128)}) %all-gather.12.cloned.1.call-update) | async-done | bytes 1048592 | tf_op jit(solution)/shard_map/all_gather | solution.py:15
  367.3 4.0 fusion
  371.3 0.0 all-gather.14.cloned.1.call-update
  371.3 0.7 copy.5
  372.0 53.0 %all-gather.14.cloned.1.call-done = f32[128,2048]{0,1:T(8,128)} async-done(((f32[128,128]{0,1:T(8,128)}), f32[128,2048]{0,1:T(8,128)}) %all-gather.14.cloned.1.call-update) | async-done | bytes 1048592 | tf_op jit(solution)/shard_map/all_gather | solution.py:44
  425.0 0.0 copy-done
  425.0 3.7 fusion.4
  (1 shorter events, 0.0 us)
Async XLA Ops:
  7.2 0.7 copy-start.3
  7.2 93.6 %all-reduce.3.cloned.1.call-start = ((), (), s32[]{:S(2)}) async-start(), calls=%async_computation | async-start | bytes 524288 | tf_op jit(solution)/shard_map/psum | solution.py:27
  35.4 106.1 %all-reduce.5.cloned.1.call-start = ((), (), s32[]{:S(2)}) async-start(), calls=%async_computation.1 | async-start | bytes 524288 | tf_op jit(solution)/shard_map/psum | solution.py:27
  100.8 0.8 copy-start.2
  100.8 124.2 %all-gather.10.cloned.1.call-start = ((), (), s32[]{:S(2)}) async-start(), calls=%async_computation.4 | async-start | bytes 1179648 | tf_op jit(solution)/shard_map/all_gather | solution.py:15
  190.6 3.9 copy-start.1
  194.5 87.3 %all-gather.8.cloned.1.call-start = ((), (), s32[]{:S(2)}) async-start(), calls=%async_computation.3 | async-start | bytes 1114112 | tf_op jit(solution)/shard_map/all_gather | solution.py:44
  195.1 138.6 %all-gather.6.cloned.1.call-start = ((), (), s32[]{:S(2)}) async-start(), calls=%async_computation.2 | async-start | bytes 1114112 | tf_op jit(solution)/shard_map/all_gather | solution.py:44
  195.7 171.6 %all-gather.12.cloned.1.call-start = ((), (), s32[]{:S(2)}) async-start(), calls=%async_computation.5 | async-start | bytes 1179648 | tf_op jit(solution)/shard_map/all_gather | solution.py:15
  289.1 135.9 %copy-start = (f32[2048,128]{0,1:T(8,128)S(1)}, f32[2048,128]{0,1:T(8,128)}, u32[]{:S(2)}) copy-start(f32[2048,128]{0,1:T(8,128)} %all-gather.10.cloned.1.call-done) | copy-start | bytes 3145732
  289.1 135.9 %all-gather.14.cloned.1.call-start = ((), (), s32[]{:S(2)}) async-start(), calls=%async_computation.6 | async-start | bytes 1114112 | tf_op jit(solution)/shard_map/all_gather | solution.py:44
Sparse Core Ops, SparseCore 0:
  35.5 65.2 all-reduce.2
  103.4 38.0 all-reduce.4
  194.6 30.4 all-gather.9
  228.3 53.5 all-gather.7
  285.0 48.6 all-gather.5
  335.4 31.8 all-gather.11
  371.4 53.5 all-gather.13
where the time goes:
time: 436 us
  waiting for transfers between devices  323 us (74%)
  blocking collectives  80.2 us (18%)
  between operations  14.9 us (3%)
  matrix products  13.2 us (3%)
    all_gather x3, waiting for transfers between devices, panels(): whole_row = lax.all_gather(factor_one, GY, axis=1, tiled=True)  154 us
    psum x2, waiting for transfers between devices, spread(): array = lax.psum(array, axis)  105 us
    all_gather x2, waiting for transfers between devices, gather_axes(): filled = lax.all_gather(filled, axes[number], axis=dim, tiled=True)  62.9 us
    psum x5, blocking collectives, over_axes(): array = lax.psum(array, axis)  45.7 us
    all_gather x1, blocking collectives, local(): panel_rows = lax.all_gather(gradient, GY, axis=1, tiled=True)  26.8 us
    dot_general x4, matrix products, matmul(): jnp.dot(leading, trailing, preferred_element_type=jnp.float32, precision=...  13.2 us
  transfers between devices with their start and end apart: 7, of which 7 were waited for; matrix products, arithmetic and copies ran while one was open for 1% of the time, Pallas kernels for 0%

commit v1 on v0

--- a/solution.py
+++ b/solution.py
@@ -30,7 +30,7 @@
 
 def over_axes(array, axes):
     for axis in axes:
-        array = lax.psum(array, axis)
+        array = jnp.sum(lax.all_gather(array, axis), axis=0)
     return array
 
 

time: 436 us -> 445 us (1.021)
  local copies, waits for them, and re-layouts: 2.25 us -> 12.9 us
    psum x5 -> x0, blocking collectives: 45.7 us -> none  [over_axes(): array = lax.psum(array, axis)]
    unnamed x0 -> x5, blocking collectives: none -> 42.5 us
    unnamed x10 -> x35, local copies, waits for them, and re-layouts: 2.25 us -> 12.9 us
where the time goes in v1:
time: 445 us
  waiting for transfers between devices  322 us (72%)
  blocking collectives  77 us (17%)
  between operations  14.9 us (3%)
  matrix products  13.2 us (3%)
  local copies, waits for them, and re-layouts  12.9 us (3%)
    all_gather x3, waiting for transfers between devices, panels(): whole_row = lax.all_gather(factor_one, GY, axis=1, tiled=True)  154 us
    psum x2, waiting for transfers between devices, spread(): array = lax.psum(array, axis)  104 us
    all_gather x2, waiting for transfers between devices, gather_axes(): filled = lax.all_gather(filled, axes[number], axis=dim, tiled=True)  62.9 us
    unnamed x5, blocking collectives  42.5 us
    all_gather x1, blocking collectives, local(): panel_rows = lax.all_gather(gradient, GY, axis=1, tiled=True)  26.8 us
    dot_general x4, matrix products, matmul(): jnp.dot(leading, trailing, preferred_element_type=jnp.float32, precision=...  13.2 us
    unnamed x35, local copies, waits for them, and re-layouts  12.9 us
  transfers between devices with their start and end apart: 7, of which 7 were waited for; matrix products, arithmetic and copies ran while one was open for 1% of the time, Pallas kernels for 0%

profile of v1, /device:TPU:1, one launch (start us, length us, event | category | flops | bytes accessed | tf_op | source)
XLA Modules:
  0.0 444.8 jit_solution(13766402503098485802)
XLA Ops:
  7.2 0.0 all-reduce.8.cloned.1.call-start
  7.2 0.7 copy-done.3
  7.9 26.8 %all_gather.56 = f32[128,512]{0,1:T(8,128)S(1)} all-gather(f32[128,32]{0,1:T(8,128)S(1)} %copy-done.3), channel_id=1, replica_groups=mesh['gx_0'=8,'gx_1'=2,'gy_0'=4,'gy_1'=2,'gy_2'=2] {'gy_0','gy_1','gy_2'}, dimensions={1}, use_global_device_ids=true | all-gather | bytes 278528 | tf_op jit(solution)/shard_map/all_gather | solution.py:65
  34.6 0.7 broadcast_select_fusion
  35.4 0.0 all-reduce.10.cloned.1.call-start
  35.4 65.4 %all-reduce.8.cloned.1.call-done = f32[128,512]{0,1:T(8,128)} async-done(((f32[128,512]{0,1:T(8,128)}), f32[128,512]{0,1:T(8,128)}) %all-reduce.8.cloned.1.call-update) | async-done | bytes 262160 | tf_op jit(solution)/shard_map/psum | solution.py:27
  100.8 0.0 all-gather.10.cloned.1.call-start
  100.9 0.8 copy-done.2
  101.6 0.1 copy.4
  101.8 0.7 copy-done.8
  102.4 0.6 dynamic-slice
  103.0 38.4 %all-reduce.10.cloned.1.call-done = f32[128,512]{0,1:T(8,128)} async-done(((f32[128,512]{0,1:T(8,128)}), f32[128,512]{0,1:T(8,128)}) %all-reduce.10.cloned.1.call-update) | async-done | bytes 262160 | tf_op jit(solution)/shard_map/psum | solution.py:27
  141.4 2.1 multiply_reduce_fusion
  143.6 1.4 dynamic-update-slice
  145.0 0.6 dynamic-slice.1
  145.6 13.9 %all-reduce = f32[8]{0:T(128)S(1)} all-reduce(f32[8]{0:T(128)S(1)} %dynamic-update-slice), channel_id=1, replica_groups=mesh['gx_0'=8,'gx_1'=2,'gy_0'=4,'gy_1'=2,'gy_2'=2] {'gx_0'}, use_global_device_ids=true, to_apply=%add | all-reduce | flops 8 | bytes 64
  159.5 0.6 reduce_sum.55
  160.1 1.4 dynamic-update-slice.1
  161.5 0.6 dynamic-slice.2
  162.1 3.8 all-reduce.1
  165.9 0.6 reduce_sum.56
  166.5 1.4 dynamic-update-slice.2
  167.9 0.6 dynamic-slice.3
  168.5 8.4 %all-reduce.2 = f32[4]{0:T(128)S(1)} all-reduce(f32[4]{0:T(128)S(1)} %dynamic-update-slice.2), channel_id=1, replica_groups=mesh['gx_0'=8,'gx_1'=2,'gy_0'=4,'gy_1'=2,'gy_2'=2] {'gy_0'}, use_global_device_ids=true, to_apply=%add.2 | all-reduce | flops 4 | bytes 32
  176.9 0.6 reduce_sum.57
  177.5 1.4 dynamic-update-slice.3
  178.9 0.6 dynamic-slice.4
  179.5 5.3 %all-reduce.3 = f32[2]{0:T(128)S(1)} all-reduce(f32[2]{0:T(128)S(1)} %dynamic-update-slice.3), channel_id=1, replica_groups=mesh['gx_0'=8,'gx_1'=2,'gy_0'=4,'gy_1'=2,'gy_2'=2] {'gy_1'}, use_global_device_ids=true, to_apply=%add.3 | all-reduce | flops 2 | bytes 16
  184.8 0.6 reduce_sum.58
  185.4 1.4 dynamic-update-slice.4
  186.8 11.1 %all-reduce.4 = f32[2]{0:T(128)S(1)} all-reduce(f32[2]{0:T(128)S(1)} %dynamic-update-slice.4), channel_id=1, replica_groups=mesh['gx_0'=8,'gx_1'=2,'gy_0'=4,'gy_1'=2,'gy_2'=2] {'gy_2'}, use_global_device_ids=true, to_apply=%add.4 | all-reduce | flops 2 | bytes 16
  197.9 0.6 reduce_sum.59
  199.2 0.6 select_subtract_fusion
  199.9 3.9 all_gather.69
  203.8 0.0 all-gather.8.cloned.1.call-start
  203.8 0.5 all-gather.8.cloned.1.call-update
  204.4 0.5 all-gather.6.cloned.1.call-update
  205.0 29.4 %all-gather.10.cloned.1.call-done = f32[2048,128]{0,1:T(8,128)} async-done(((f32[256,128]{0,1:T(8,128)}), f32[2048,128]{0,1:T(8,128)}) %all-gather.10.cloned.1.call-update) | async-done | bytes 1048592 | tf_op jit(solution)/shard_map/all_gather | solution.py:15
  234.3 56.8 %all-gather.8.cloned.1.call-done = f32[128,2048]{0,1:T(8,128)} async-done(((f32[128,128]{0,1:T(8,128)}), f32[128,2048]{0,1:T(8,128)}) %all-gather.8.cloned.1.call-update) | async-done | bytes 1048592 | tf_op jit(solution)/shard_map/all_gather | solution.py:44
  291.1 3.4 fusion.3
  294.5 3.9 all_gather.71
  298.4 0.0 all-gather.14.cloned.1.call-start
  298.5 44.5 %all-gather.6.cloned.1.call-done = f32[128,2048]{0,1:T(8,128)} async-done(((f32[128,128]{0,1:T(8,128)}), f32[128,2048]{0,1:T(8,128)}) %all-gather.6.cloned.1.call-update) | async-done | bytes 1048592 | tf_op jit(solution)/shard_map/all_gather | solution.py:44
  343.0 33.6 %all-gather.12.cloned.1.call-done = f32[2048,128]{1,0:T(8,128)} async-done(((f32[256,128]{1,0:T(8,128)}), f32[2048,128]{1,0:T(8,128)}) %all-gather.12.cloned.1.call-update) | async-done | bytes 1048592 | tf_op jit(solution)/shard_map/all_gather | solution.py:15
  376.6 4.0 fusion
  380.6 0.7 copy.5
  381.3 53.0 %all-gather.14.cloned.1.call-done = f32[128,2048]{0,1:T(8,128)} async-done(((f32[128,128]{0,1:T(8,128)}), f32[128,2048]{0,1:T(8,128)}) %all-gather.14.cloned.1.call-update) | async-done | bytes 1048592 | tf_op jit(solution)/shard_map/all_gather | solution.py:44
  434.3 3.7 fusion.4
  (28 shorter events, 0.2 us)
Async XLA Ops:
  7.2 0.7 copy-start.3
  7.2 93.6 %all-reduce.8.cloned.1.call-start = ((), (), s32[]{:S(2)}) async-start(), calls=%async_computation | async-start | bytes 524288 | tf_op jit(solution)/shard_map/psum | solution.py:27
  35.4 106.1 %all-reduce.10.cloned.1.call-start = ((), (), s32[]{:S(2)}) async-start(), calls=%async_computation.1 | async-start | bytes 524288 | tf_op jit(solution)/shard_map/psum | solution.py:27
  100.8 0.8 copy-start.2
  100.8 133.5 %all-gather.10.cloned.1.call-start = ((), (), s32[]{:S(2)}) async-start(), calls=%async_computation.4 | async-start | bytes 1179648 | tf_op jit(solution)/shard_map/all_gather | solution.py:15
  101.7 0.7 copy-start.8
  143.6 1.4 copy-start.7
  160.1 1.4 copy-start.6
  166.5 1.4 copy-start.5
  177.5 1.4 copy-start.4
  199.9 3.9 copy-start.1
  203.8 87.3 %all-gather.8.cloned.1.call-start = ((), (), s32[]{:S(2)}) async-start(), calls=%async_computation.3 | async-start | bytes 1114112 | tf_op jit(solution)/shard_map/all_gather | solution.py:44
  204.3 138.6 %all-gather.6.cloned.1.call-start = ((), (), s32[]{:S(2)}) async-start(), calls=%async_computation.2 | async-start | bytes 1114112 | tf_op jit(solution)/shard_map/all_gather | solution.py:44
  204.9 171.6 %all-gather.12.cloned.1.call-start = ((), (), s32[]{:S(2)}) async-start(), calls=%async_computation.5 | async-start | bytes 1179648 | tf_op jit(solution)/shard_map/all_gather | solution.py:15
  298.4 135.9 %copy-start = (f32[2048,128]{0,1:T(8,128)S(1)}, f32[2048,128]{0,1:T(8,128)}, u32[]{:S(2)}) copy-start(f32[2048,128]{0,1:T(8,128)} %all-gather.10.cloned.1.call-done) | copy-start | bytes 3145732
  298.4 135.9 %all-gather.14.cloned.1.call-start = ((), (), s32[]{:S(2)}) async-start(), calls=%async_computation.6 | async-start | bytes 1114112 | tf_op jit(solution)/shard_map/all_gather | solution.py:44
Sparse Core Ops, SparseCore 0:
  35.5 65.2 all-reduce.7
  103.4 38.0 all-reduce.9
  203.9 30.4 all-gather.9
  237.5 53.5 all-gather.7
  294.3 48.6 all-gather.5
  344.6 31.8 all-gather.11
  380.7 53.5 all-gather.13
